TPU v7x, 32 devices: a whole 2x2x4 slice. The times are simulated.
32 devices in a mesh: blk: 8 (over z, y), sp: 4 (over x, core).
Axes of the slice: x: 2, y: 2, z: 4, core: 2. Of those that a mesh axis runs over, the one named last changes fastest.
Arguments:
- tokens: bfloat16 [4096, 2304], P(('blk', 'sp')), may hold values from -6 to 6
- w_qkv: bfloat16 [4096, 2304], replicated, may hold values from -5 to 5
- w_out: bfloat16 [2048, 2304], replicated, may hold values from -0.125 to 0.125
- gains: float32 [4, 2304], replicated, may hold values from 0.1 to 1.9
- w_ffn: bfloat16 [9216, 3, 2304], P('blk'), may hold values from -0.125 to 0.125
- cotangent: bfloat16 [4096, 2304], P(('blk', 'sp')), may hold values from -6 to 6
Outputs:
- block_out: bfloat16 [4096, 2304], P(('blk', 'sp'))
- tokens_grad: bfloat16 [4096, 2304], P(('blk', 'sp'))
- qkv_grad: float32 [4096, 2304], P(('sp', 'blk'))
- out_grad: float32 [2048, 2304], P(('sp', 'blk'))
- gains_grad: float32 [4, 2304], P(None, ('sp', 'blk'))
- ffn_grad: float32 [9216, 3, 2304], P(('blk', 'sp'))
All inputs are finite; a program needn't handle non-finite values.
Results may differ from a plain program's by a relative error of at most 0.025.
Values may be sent and summed in bfloat16 or wider, within the bound.
A program may use at most 320 MiB of HBM per device.

v0:
```python
import math
import jax
import jax.numpy as jnp
from jax import lax
from jax.sharding import PartitionSpec as P

HEADS = 8
KV_HEADS = 4
HEAD = 256
NORM_EPSILON = 1e-06
CAP_VALUE = 50.0
GELU_SCALE = 0.7978845608028654
GELU_CUBIC = 0.044715


def norm_parts(values):
    inverse = lax.rsqrt(jnp.mean(values * values, axis=-1, keepdims=True) + NORM_EPSILON)
    return (values * inverse, inverse)


def norm_back(grad_y, normed, inverse, gain):
    grad_n = grad_y * gain
    grad_v = inverse * (grad_n - normed * jnp.mean(grad_n * normed, axis=-1, keepdims=True))
    return (grad_v, jnp.sum(grad_y * normed, axis=0))


def gelu_value(values):
    return (
        0.5
        * values
        * (1.0 + jnp.tanh(GELU_SCALE * (values + GELU_CUBIC * values * values * values)))
    )


def gelu_slope(values):
    bent = jnp.tanh(GELU_SCALE * (values + GELU_CUBIC * values * values * values))
    return 0.5 * (1.0 + bent) + 0.5 * values * (1.0 - bent * bent) * GELU_SCALE * (
        1.0 + 3.0 * GELU_CUBIC * values * values
    )


def contract_last(left, right):
    return lax.dot_general(
        left, right, (((1,), (1,)), ((), ())), preferred_element_type=jnp.float32
    )


def body(tokens, w_qkv, w_out, gains, w_ffn, cotangent):
    row_count = tokens.shape[0]
    groups = lax.axis_size("sp")
    cycle_size = lax.axis_size("blk")
    heads_here = HEADS // groups
    kv_here = KV_HEADS // groups
    group_ratio = HEADS // KV_HEADS
    query_width = HEADS * HEAD
    score_scale = HEAD ** (-0.5)
    source = tokens.astype(jnp.float32)
    normed_in, inverse_in = norm_parts(source)
    act_in = (normed_in * gains[0]).astype(jnp.bfloat16)
    projected = (
        contract_last(act_in, w_qkv)
        .astype(jnp.bfloat16)
        .reshape(row_count, KV_HEADS, group_ratio + 2, HEAD)
    )
    head_data = lax.all_to_all(projected, "sp", split_axis=1, concat_axis=0, tiled=True)
    block_rows = head_data.shape[0]
    query_group = head_data[:, :, :group_ratio]
    key_heads = head_data[:, :, group_ratio]
    value_heads = head_data[:, :, group_ratio + 1]
    first_query = lax.axis_index("blk") * block_rows
    last_query = first_query + block_rows - 1
    query_places = first_query + jnp.arange(block_rows, dtype=jnp.int32)

    def tile_scores(key_tile, tile_first):
        tile_rows = key_tile.shape[0]
        raw = jnp.einsum(
            "qkgd,rkd->kgqr", query_group, key_tile, preferred_element_type=jnp.float32
        )
        squashed = jnp.tanh(raw * score_scale / CAP_VALUE)
        allowed = (tile_first + jnp.arange(tile_rows, dtype=jnp.int32))[None, :] <= query_places[
            :, None
        ]
        weights = jnp.where(allowed, jnp.exp(CAP_VALUE * squashed), 0.0)
        return (weights, squashed)

    def run_tiles(state_now, pieces, tile_step):
        key_piece, value_piece = pieces
        piece_rows = key_piece.shape[0]
        tile_rows = math.gcd(piece_rows, block_rows)
        tile_count = piece_rows // tile_rows
        key_tiles = key_piece.reshape(tile_count, tile_rows, kv_here, HEAD)
        value_tiles = value_piece.reshape(tile_count, tile_rows, kv_here, HEAD)

        def one_tile(state_in, items):
            key_tile, value_tile, tile_index = items
            return (tile_step(state_in, key_tile, value_tile, tile_index * tile_rows), None)

        state_out, unused = lax.scan(
            one_tile, state_now, (key_tiles, value_tiles, jnp.arange(tile_count, dtype=jnp.int32))
        )
        return state_out

    def forward_step(state_in, key_tile, value_tile, tile_first):

        def forward_compute(state_old):
            totals_old, summed_old = state_old
            weights, squashed = tile_scores(key_tile, tile_first)
            totals_new = totals_old + jnp.sum(weights, axis=-1)
            summed_new = summed_old + jnp.einsum(
                "kgqr,rkd->qkgd",
                weights.astype(jnp.bfloat16),
                value_tile,
                preferred_element_type=jnp.float32,
            )
            return (totals_new, summed_new)

        return lax.cond(
            tile_first <= last_query, forward_compute, lambda state_old: state_old, state_in
        )

    zero_totals = jnp.zeros((kv_here, group_ratio, block_rows), jnp.float32)
    zero_summed = jnp.zeros((block_rows, kv_here, group_ratio, HEAD), jnp.float32)
    totals, summed = run_tiles(
        (zero_totals, zero_summed),
        (
            lax.all_gather(key_heads, "blk", axis=0, tiled=True),
            lax.all_gather(value_heads, "blk", axis=0, tiled=True),
        ),
        forward_step,
    )
    totals_rows = jnp.transpose(totals, (2, 0, 1))[..., None]
    attended = summed / totals_rows
    attended_low = attended.reshape(block_rows, heads_here, HEAD).astype(jnp.bfloat16)
    attended_tokens = lax.all_to_all(
        attended_low, "sp", split_axis=0, concat_axis=1, tiled=True
    ).reshape(row_count, query_width)
    attn = jnp.dot(attended_tokens, w_out, preferred_element_type=jnp.float32)
    normed_attn, inverse_attn = norm_parts(attn)
    middle = source + normed_attn * gains[1]
    normed_mid, inverse_mid = norm_parts(middle)
    act_ffn = (normed_mid * gains[2]).astype(jnp.bfloat16)
    w_in = w_ffn[:, :2, :]
    w_down = w_ffn[:, 2, :]
    gate_up = jnp.einsum(
        "td,fkd->tkf",
        lax.all_gather(act_ffn, "blk", axis=0, tiled=True),
        w_in,
        preferred_element_type=jnp.float32,
    )
    hidden = (gelu_value(gate_up[:, 0]) * gate_up[:, 1]).astype(jnp.bfloat16)
    hidden_all = hidden
    part = hidden_all
    ffn_out = lax.psum_scatter(
        jnp.dot(part, w_down, preferred_element_type=jnp.float32).astype(jnp.bfloat16),
        "blk",
        scatter_dimension=0,
        tiled=True,
    ).astype(jnp.float32)
    normed_ffn, inverse_ffn = norm_parts(ffn_out)
    result = middle + normed_ffn * gains[3]
    grad_out = cotangent.astype(jnp.float32)
    grad_ffn_f, gain_grad3 = norm_back(grad_out, normed_ffn, inverse_ffn, gains[3])
    grad_ffn = grad_ffn_f.astype(jnp.bfloat16)
    act_piece = lax.all_gather(act_ffn, "blk", axis=0, tiled=True)
    grad_piece = lax.all_gather(grad_ffn, "blk", axis=0, tiled=True)
    gate_up = jnp.einsum("td,fkd->tkf", act_piece, w_in, preferred_element_type=jnp.float32)
    hidden = (gelu_value(gate_up[:, 0]) * gate_up[:, 1]).astype(jnp.bfloat16)
    grad_hidden = contract_last(grad_piece, w_down)
    grad_gate = grad_hidden * gate_up[:, 1] * gelu_slope(gate_up[:, 0])
    grad_up = grad_hidden * gelu_value(gate_up[:, 0])
    grad_pair = jnp.stack([grad_gate, grad_up], axis=1).astype(jnp.bfloat16)
    in_part = jnp.einsum("tkf,td->fkd", grad_pair, act_piece, preferred_element_type=jnp.float32)
    down_part = jnp.einsum("tf,td->fd", hidden, grad_piece, preferred_element_type=jnp.float32)
    weight_sum = jnp.concatenate([in_part, down_part[:, None, :]], axis=1)
    part = grad_pair
    grad_act_ffn = lax.psum_scatter(
        jnp.einsum("tkf,fkd->td", part, w_in, preferred_element_type=jnp.float32).astype(
            jnp.bfloat16
        ),
        "blk",
        scatter_dimension=0,
        tiled=True,
    ).astype(jnp.float32)
    grad_norm_mid, gain_grad2 = norm_back(grad_act_ffn, normed_mid, inverse_mid, gains[2])
    grad_middle = grad_out + grad_norm_mid
    grad_attn_f, gain_grad1 = norm_back(grad_middle, normed_attn, inverse_attn, gains[1])
    grad_attn = grad_attn_f.astype(jnp.bfloat16)
    out_term = jnp.einsum(
        "tc,td->cd", attended_tokens, grad_attn, preferred_element_type=jnp.float32
    )
    grad_attended = (
        contract_last(grad_attn, w_out).astype(jnp.bfloat16).reshape(row_count, HEADS, HEAD)
    )
    grad_heads = lax.all_to_all(
        grad_attended, "sp", split_axis=1, concat_axis=0, tiled=True
    ).reshape(block_rows, kv_here, group_ratio, HEAD)
    grad_heads_f = grad_heads.astype(jnp.float32)
    scaled = (grad_heads_f / totals_rows).astype(jnp.bfloat16)
    row_delta = jnp.transpose(
        jnp.sum(grad_heads_f * attended, axis=-1) / totals_rows[..., 0], (1, 2, 0)
    )

    def backward_step(state_in, key_tile, value_tile, tile_first):
        tile_rows = key_tile.shape[0]

        def backward_compute(state_old):
            grad_query, grad_keys, grad_values = state_old
            weights, squashed = tile_scores(key_tile, tile_first)
            grad_weights = (
                jnp.einsum("qkgd,rkd->kgqr", scaled, value_tile, preferred_element_type=jnp.float32)
                - row_delta[..., None]
            )
            grad_raw = (weights * grad_weights * (1.0 - squashed * squashed) * score_scale).astype(
                jnp.bfloat16
            )
            grad_query = grad_query + jnp.einsum(
                "kgqr,rkd->qkgd", grad_raw, key_tile, preferred_element_type=jnp.float32
            )
            key_part = jnp.einsum(
                "kgqr,qkgd->rkd", grad_raw, query_group, preferred_element_type=jnp.float32
            )
            value_part = jnp.einsum(
                "kgqr,qkgd->rkd",
                weights.astype(jnp.bfloat16),
                scaled,
                preferred_element_type=jnp.float32,
            )
            old_keys = lax.dynamic_slice_in_dim(grad_keys, tile_first, tile_rows, 0)
            grad_keys = lax.dynamic_update_slice_in_dim(
                grad_keys, old_keys + key_part, tile_first, 0
            )
            old_values = lax.dynamic_slice_in_dim(grad_values, tile_first, tile_rows, 0)
            grad_values = lax.dynamic_update_slice_in_dim(
                grad_values, old_values + value_part, tile_first, 0
            )
            return (grad_query, grad_keys, grad_values)

        return lax.cond(
            tile_first <= last_query, backward_compute, lambda state_old: state_old, state_in
        )

    start_back = (
        jnp.zeros((block_rows, kv_here, group_ratio, HEAD), jnp.float32),
        jnp.zeros((cycle_size * block_rows, kv_here, HEAD), jnp.float32),
        jnp.zeros((cycle_size * block_rows, kv_here, HEAD), jnp.float32),
    )
    grad_query, grad_keys_all, grad_values_all = run_tiles(
        start_back,
        (
            lax.all_gather(key_heads, "blk", axis=0, tiled=True),
            lax.all_gather(value_heads, "blk", axis=0, tiled=True),
        ),
        backward_step,
    )
    grad_keys, grad_values = (
        lax.psum_scatter(
            grad_keys_all.astype(jnp.bfloat16), "blk", scatter_dimension=0, tiled=True
        ).astype(jnp.float32),
        lax.psum_scatter(
            grad_values_all.astype(jnp.bfloat16), "blk", scatter_dimension=0, tiled=True
        ).astype(jnp.float32),
    )
    grad_proj_heads = jnp.concatenate(
        [grad_query, grad_keys[:, :, None], grad_values[:, :, None]], axis=2
    ).astype(jnp.bfloat16)
    grad_proj_tokens = lax.all_to_all(
        grad_proj_heads, "sp", split_axis=0, concat_axis=1, tiled=True
    )
    grad_projected = grad_proj_tokens.reshape(row_count, w_qkv.shape[0])
    grad_act_in = jnp.dot(grad_projected, w_qkv, preferred_element_type=jnp.float32)
    grad_source, gain_grad0 = norm_back(grad_act_in, normed_in, inverse_in, gains[0])
    tokens_grad = (grad_middle + grad_source).astype(jnp.bfloat16)
    gains_term = jnp.stack([gain_grad0, gain_grad1, gain_grad2, gain_grad3], axis=0)
    qkv_term = jnp.einsum("tc,td->cd", grad_projected, act_in, preferred_element_type=jnp.float32)
    ffn_grad, qkv_part, out_part, gains_part = (
        lax.psum_scatter(
            weight_sum.astype(jnp.bfloat16), "sp", scatter_dimension=0, tiled=True
        ).astype(jnp.float32),
        lax.psum_scatter(
            qkv_term.astype(jnp.bfloat16), "sp", scatter_dimension=0, tiled=True
        ).astype(jnp.float32),
        lax.psum_scatter(
            out_term.astype(jnp.bfloat16), "sp", scatter_dimension=0, tiled=True
        ).astype(jnp.float32),
        lax.psum_scatter(
            gains_term.astype(jnp.bfloat16), "sp", scatter_dimension=1, tiled=True
        ).astype(jnp.float32),
    )
    qkv_grad, out_grad, gains_grad = (
        lax.psum_scatter(
            qkv_part.astype(jnp.bfloat16), "blk", scatter_dimension=0, tiled=True
        ).astype(jnp.float32),
        lax.psum_scatter(
            out_part.astype(jnp.bfloat16), "blk", scatter_dimension=0, tiled=True
        ).astype(jnp.float32),
        lax.psum_scatter(
            gains_part.astype(jnp.bfloat16), "blk", scatter_dimension=1, tiled=True
        ).astype(jnp.float32),
    )
    return (result.astype(jnp.bfloat16), tokens_grad, qkv_grad, out_grad, gains_grad, ffn_grad)


def solution(mesh):
    return jax.shard_map(
        body,
        mesh=mesh,
        in_specs=(
            P(("blk", "sp"), None),
            P(),
            P(),
            P(),
            P("blk", None, None),
            P(("blk", "sp"), None),
        ),
        out_specs=(
            P(("blk", "sp"), None),
            P(("blk", "sp"), None),
            P(("sp", "blk"), None),
            P(("sp", "blk"), None),
            P(None, ("sp", "blk")),
            P(("blk", "sp"), None, None),
        ),
        check_vma=False,
    )
```

profile of v0, /device:TPU:0, one launch (start us, length us, event | category | flops | bytes accessed | tf_op | source)
XLA Modules:
  0.0 1483.3 jit_solution(1569440908455529645)
XLA Ops:
  9.5 12.8 convolution_convert_fusion.5
  23.5 18.5 %all_to_all.57 = bf16[128,4,4,256]{3,2,0,1:T(4,128)(2,1)S(1)} all-to-all(bf16[128,4,4,256]{3,2,0,1:T(4,128)(2,1)S(1)} %copy.95), channel_id=1, replica_groups=mesh['blk'=8,'sp'=4] {'sp'}, dimensions={1} | all-to-all | bytes 2097152 | tf_op jit(solution)/shard_map/all_to_all | solution.py:65
  43.9 48.7 %all-gather.13.cloned.1.call-done = bf16[4096,1,1,256]{3,0,2,1:T(8,128)(2,1)} async-done(((bf16[512,1,1,256]{3,0,2,1:T(8,128)(2,1)}), bf16[4096,1,1,256]{3,0,2,1:T(8,128)(2,1)}) %all-gather.13.cloned.1.call-update) | async-done | bytes 2097168 | tf_op jit(solution)/shard_map/all_gather | solution.py:127
  96.5 46.4 %all-gather.11.cloned.1.call-done = bf16[4096,1,1,256]{3,0,2,1:T(8,128)(2,1)} async-done(((bf16[512,1,1,256]{3,0,2,1:T(8,128)(2,1)}), bf16[4096,1,1,256]{3,0,2,1:T(8,128)(2,1)}) %all-gather.11.cloned.1.call-update) | async-done | bytes 2097168 | tf_op jit(solution)/shard_map/all_gather | solution.py:126
  143.1 13.9 while.28
  159.4 11.3 all_to_all.58
  178.2 102.1 %all-gather.7.cloned.1.call-done = bf16[1024,2304]{1,0:T(8,128)(2,1)} async-done(((bf16[128,2304]{1,0:T(8,128)(2,1)}), bf16[1024,2304]{1,0:T(8,128)(2,1)}) %all-gather.7.cloned.1.call-update) | async-done | bytes 4718608 | tf_op jit(solution)/shard_map/all_gather | solution.py:146
  280.3 16.6 %fusion.51 = f32[1024,2,1152]{2,0,1:T(8,128)S(1)} fusion(bf16[1152,3,2304]{2,0,1:T(8,128)(2,1)} %param.18, bf16[1024,2304]{1,0:T(8,128)(2,1)} %all-gather.7.cloned.1.call-done), kind=kOutput, calls=%fused_computation.73 | convolution fusion | flops 10871635968 | bytes 24772608 | tf_op jit(solution)/shard_map/td,fkd->tkf/dot_general | solution.py:144
  300.6 11.3 convolution_convert_fusion.4
  311.9 94.1 %reduce-scatter.16.cloned.1.call-done = bf16[128,2304]{1,0:T(8,128)(2,1)} async-done(((bf16[1024,2304]{1,0:T(8,128)(2,1)}), bf16[128,2304]{1,0:T(8,128)(2,1)}) %reduce-scatter.16.cloned.1.call-update) | async-done | bytes 589840 | tf_op jit(solution)/shard_map/reduce_scatter | solution.py:153
  411.6 78.7 %all-gather.9.cloned.1.call-done = bf16[1024,2304]{1,0:T(8,128)(2,1)} async-done(((bf16[128,2304]{1,0:T(8,128)(2,1)}), bf16[1024,2304]{1,0:T(8,128)(2,1)}) %all-gather.9.cloned.1.call-update) | async-done | bytes 4718608 | tf_op jit(solution)/shard_map/all_gather | solution.py:165
  490.3 14.7 fusion.85
  507.1 14.7 bitcast_convert_fusion
  521.9 94.1 %reduce-scatter.18.cloned.1.call-done = bf16[128,2304]{1,0:T(8,128)(2,1)} async-done(((bf16[1024,2304]{1,0:T(8,128)(2,1)}), bf16[128,2304]{1,0:T(8,128)(2,1)}) %reduce-scatter.18.cloned.1.call-update) | async-done | bytes 589840 | tf_op jit(solution)/shard_map/reduce_scatter | solution.py:176
  633.5 8.4 all-to-all-done.2
  650.0 27.3 %while.29 = (s32[]{:T(128)}, f32[512,1,2,256]{0,3,2,1:T(8,128)S(1)}, f32[4096,1,256]{2,0,1:T(8,128)}, f32[4096,1,256]{2,0,1:T(8,128)}, s32[8]{0:T(128)S(1)}, /*i...) while((s32[]{:T(128)}, ...), condition=%wide.region_18.19_spmd.clone, body=%wide.region_15.18_spmd.clone.sunk | while | flops 1350304768 | bytes 27805592 | solution.py:98
  651.3 16.7 %conditional.7 = ((f32[512,1,2,256]{0,3,2,1:T(8,128)S(1)}, f32[4096,1,256]{2,0,1:T(8,128)}, f32[4096,1,256]{2,0,1:T(8,128)})) conditional(s32[]{:T(128)} %convert_element_type.314, (f32[512,1,2,256]{0,3,2,1:T(8,128)S(1)}, f32[4096,1,256]{2,0,1:T(8,128)}, f32[4096,1,256]{2,0,1:T(8,128)}) %tuple.108, (bf16[8,512,1,256]{3,1,2,0:T(8,128)(2,1)}, ...), branch_computations={%region_16.16_spmd, %region_17.17_spmd} | conditional | flops 1350304768 | bytes 27803254 | solution.py:238
  691.7 171.7 %reduce-scatter.20.cloned.1.call-done = bf16[512,1,256]{2,0,1:T(8,128)(2,1)} async-done(((bf16[4096,1,256]{2,0,1:T(8,128)(2,1)}), bf16[512,1,256]{2,0,1:T(8,128)(2,1)}) %reduce-scatter.20.cloned.1.call-update) | async-done | bytes 262160 | tf_op jit(solution)/shard_map/reduce_scatter | solution.py:256
  864.7 70.2 %reduce-scatter.22.cloned.1.call-done = bf16[512,1,256]{2,0,1:T(8,128)(2,1)} async-done(((bf16[4096,1,256]{2,0,1:T(8,128)(2,1)}), bf16[512,1,256]{2,0,1:T(8,128)(2,1)}) %reduce-scatter.22.cloned.1.call-update) | async-done | bytes 262160 | tf_op jit(solution)/shard_map/reduce_scatter | solution.py:259
  938.1 17.2 %all_to_all.59 = bf16[512,1,4,256]{3,2,1,0:T(4,128)(2,1)S(1)} all-to-all(bf16[512,1,4,256]{3,2,1,0:T(4,128)(2,1)S(1)} %pad_maximum_fusion.4), channel_id=1, replica_groups=mesh['blk'=8,'sp'=4] {'sp'}, dimensions={0} | all-to-all | bytes 2097152 | tf_op jit(solution)/shard_map/all_to_all | solution.py:266
  958.0 9.2 convolution_convert_fusion
  967.3 13.2 fusion.46
  980.5 17.4 %fusion.45 = bf16[1152,2,2304]{0,2,1:T(8,128)(2,1)} fusion(bf16[1024,2304]{1,0:T(8,128)(2,1)} %all-gather.7.cloned.1.call-done, bf16[1024,1,1152]{2,0,1:T(8,128)(2,1)} %copy-done.22, bf16[1024,1,1152]{2,0,1:T(8,128)(2,1)} %copy-done.21), kind=kOutput, calls=%fused_computation.61 | convolution fusion | flops 10886381568 | bytes 20054016 | tf_op jit(solution)/shard_map/tkf,td->fkd/dot_general | solution.py:172
  1004.5 13.4 pad_maximum_fusion
  1017.9 21.6 %copy.131 = bf16[1152,6912]{1,0:T(8,128)(2,1)} copy(bf16[1152,6912]{0,1:T(8,128)(2,1)} %bitcast.253) | data formatting | bytes 31850496
  1040.3 114.6 %reduce-scatter.24.cloned.1.call-done = bf16[1024,2304]{1,0:T(8,128)(2,1)} async-done(((bf16[4096,2304]{1,0:T(8,128)(2,1)}), bf16[1024,2304]{1,0:T(8,128)(2,1)}) %reduce-scatter.24.cloned.1.call-update) | async-done | bytes 4718608 | tf_op jit(solution)/shard_map/reduce_scatter | solution.py:279
  1159.3 20.8 %reduce-scatter.32.cloned.1.call-done = bf16[576,4]{1,0:T(8,128)(2,1)} async-done(((bf16[2304,4]{1,0:T(8,128)(2,1)}), bf16[576,4]{1,0:T(8,128)(2,1)}) %reduce-scatter.32.cloned.1.call-update) | async-done | bytes 4624
  1181.1 21.7 %all-reduce = bf16[4,576]{1,0:T(4,128)(2,1)S(1)} all-reduce(bf16[4,576]{1,0:T(4,128)(2,1)S(1)} %copy.126), channel_id=13, replica_groups=mesh['blk'=8,'sp'=4] {'blk'}, use_global_device_ids=true, to_apply=%region_31.32.clone | all-reduce | flops 2304 | bytes 9216
  1203.5 99.2 %reduce-scatter.34.cloned.1.call-done = bf16[288,6912]{1,0:T(8,128)(2,1)} async-done(((bf16[1152,6912]{1,0:T(8,128)(2,1)}), bf16[288,6912]{1,0:T(8,128)(2,1)}) %reduce-scatter.34.cloned.1.call-update) | async-done | bytes 3981328
  1309.2 7.3 copy.117
  1316.6 59.1 %reduce-scatter.30.cloned.1.call-done = bf16[64,2304]{1,0:T(8,128)(2,1)} async-done(((bf16[512,2304]{1,0:T(8,128)(2,1)}), bf16[64,2304]{1,0:T(8,128)(2,1)}) %reduce-scatter.30.cloned.1.call-update) | async-done | bytes 294928 | tf_op jit(solution)/shard_map/reduce_scatter | solution.py:293
  1377.5 96.6 %reduce-scatter.26.cloned.1.call-done = bf16[128,2304]{1,0:T(8,128)(2,1)} async-done(((bf16[1024,2304]{1,0:T(8,128)(2,1)}), bf16[128,2304]{1,0:T(8,128)(2,1)}) %reduce-scatter.26.cloned.1.call-update) | async-done | bytes 589840 | tf_op jit(solution)/shard_map/reduce_scatter | solution.py:290
  (216 shorter events, 134.6 us)
Async XLA Ops:
  7.2 85.4 %all-gather.13.cloned.1.call-start = ((), (), s32[]{:S(2)}) async-start(), calls=%async_computation.25 | async-start | bytes 2359296 | tf_op jit(solution)/shard_map/all_gather | solution.py:127
  8.2 14.1 copy-start.15
  9.5 12.8 copy-start.17
  43.0 99.9 %all-gather.11.cloned.1.call-start = ((), (), s32[]{:S(2)}) async-start(), calls=%async_computation.24 | async-start | bytes 2359296 | tf_op jit(solution)/shard_map/all_gather | solution.py:126
  43.8 236.5 %all-gather.7.cloned.1.call-start = ((), (), s32[]{:S(2)}) async-start(), calls=%async_computation.14 | async-start | bytes 5308416 | tf_op jit(solution)/shard_map/all_gather | solution.py:146
  171.1 5.4 copy-start.7
  171.1 5.4 copy-start.1
  177.9 228.1 %reduce-scatter.16.cloned.1.call-start = ((), (), s32[]{:S(2)}) async-start(), calls=%async_computation.15 | async-start | bytes 5308416 | tf_op jit(solution)/shard_map/reduce_scatter | solution.py:153
  296.9 3.7 copy-start.20
  311.8 95.5 %copy-start.11 = (bf16[128,2304]{1,0:T(8,128)(2,1)S(1)}, bf16[128,2304]{1,0:T(8,128)(2,1)}, u32[]{:S(2)}) copy-start(bf16[128,2304]{1,0:T(8,128)(2,1)} %param.19) | copy-start | bytes 1769476
  311.9 178.4 %all-gather.9.cloned.1.call-start = ((), (), s32[]{:S(2)}) async-start(), calls=%async_computation.16 | async-start | bytes 5308416 | tf_op jit(solution)/shard_map/all_gather | solution.py:165
  411.2 204.8 %reduce-scatter.18.cloned.1.call-start = ((), (), s32[]{:S(2)}) async-start(), calls=%async_computation.17 | async-start | bytes 5308416 | tf_op jit(solution)/shard_map/reduce_scatter | solution.py:176
  521.8 95.7 %copy-start.6 = (bf16[128,2304]{1,0:T(8,128)(2,1)S(1)}, bf16[128,2304]{1,0:T(8,128)(2,1)}, u32[]{:S(2)}) copy-start(bf16[128,2304]{1,0:T(8,128)(2,1)} %reduce-scatter.16.cloned.1.call-done) | copy-start | bytes 1769476
  621.8 7.0 copy-start.9
  628.8 13.7 copy-start.12
  628.9 13.7 copy-start.14
  629.7 12.3 all-to-all-start.2
  633.2 230.2 %reduce-scatter.20.cloned.1.call-start = ((), (), s32[]{:S(2)}) async-start(), calls=%async_computation.18 | async-start | bytes 2359296 | tf_op jit(solution)/shard_map/reduce_scatter | solution.py:256
  681.0 253.9 %reduce-scatter.22.cloned.1.call-start = ((), (), s32[]{:S(2)}) async-start(), calls=%async_computation.19 | async-start | bytes 2359296 | tf_op jit(solution)/shard_map/reduce_scatter | solution.py:259
  684.8 354.8 %reduce-scatter.28.cloned.1.call-start = ((), (), s32[]{:S(2)}) async-start(), calls=%async_computation.22 | async-start | bytes 11796480 | tf_op jit(solution)/shard_map/reduce_scatter | solution.py:282
  691.0 463.9 %reduce-scatter.24.cloned.1.call-start = ((), (), s32[]{:S(2)}) async-start(), calls=%async_computation.20 | async-start | bytes 23592960 | tf_op jit(solution)/shard_map/reduce_scatter | solution.py:279
  955.2 2.8 copy-start.18
  958.0 9.2 copy-start.3
  967.2 212.9 %reduce-scatter.32.cloned.1.call-start = ((), (), s32[]{:S(2)}) async-start(), calls=%async_computation.26 | async-start | bytes 737280
  967.3 30.7 %slice-start = ((s8[18874368]{0:T(1024)(128)(4,1)}), s8[4194304]{0:T(1024)(128)(4,1)S(1)}, s32[]{:S(2)}) async-start(s8[18874368]{0:T(1024)(128)(4,1)} %bitcast.251), calls=%async_computation.28 | async-start | bytes 8388608
  967.3 30.7 %slice-start.1 = ((s8[18874368]{0:T(1024)(128)(4,1)}), s8[4194304]{0:T(1024)(128)(4,1)S(1)}, s32[]{:S(2)}) async-start(s8[18874368]{0:T(1024)(128)(4,1)} %bitcast.251), calls=%async_computation.29 | async-start | bytes 8388608
  980.5 17.5 %slice-start.2 = ((s8[18874368]{0:T(1024)(128)(4,1)}), s8[4194304]{0:T(1024)(128)(4,1)S(1)}, s32[]{:S(2)}) async-start(s8[18874368]{0:T(1024)(128)(4,1)} %bitcast.251), calls=%async_computation.30 | async-start | bytes 8388608
  980.5 17.5 %slice-start.3 = ((s8[18874368]{0:T(1024)(128)(4,1)}), s8[4194304]{0:T(1024)(128)(4,1)S(1)}, s32[]{:S(2)}) async-start(s8[18874368]{0:T(1024)(128)(4,1)} %bitcast.251), calls=%async_computation.31 | async-start | bytes 8388608
  980.5 17.5 %slice-start.4 = ((s8[18874368]{0:T(1024)(128)(4,1)}), s8[2097152]{0:T(1024)(128)(4,1)S(1)}, s32[]{:S(2)}) async-start(s8[18874368]{0:T(1024)(128)(4,1)} %bitcast.251), calls=%async_computation.32 | async-start | bytes 4194304
  1004.4 298.3 %reduce-scatter.34.cloned.1.call-start = ((), (), s32[]{:S(2)}) async-start(), calls=%async_computation.27 | async-start | bytes 19906560
  1039.5 336.2 %reduce-scatter.30.cloned.1.call-start = ((), (), s32[]{:S(2)}) async-start(), calls=%async_computation.23 | async-start | bytes 2654208 | tf_op jit(solution)/shard_map/reduce_scatter | solution.py:293
  1040.3 433.9 %reduce-scatter.26.cloned.1.call-start = ((), (), s32[]{:S(2)}) async-start(), calls=%async_computation.21 | async-start | bytes 5308416 | tf_op jit(solution)/shard_map/reduce_scatter | solution.py:290
  (11 other events, 18.5 us)
Sparse Core Ops, SparseCore 0:
  43.2 49.3 all-gather.12
  95.3 47.6 all-gather.10
  178.1 102.1 all-gather.6
  312.0 94.0 reduce-scatter.15
  411.3 78.9 all-gather.8
  522.0 93.9 reduce-scatter.17
  681.1 182.1 reduce-scatter.19
  867.4 67.4 reduce-scatter.21
  937.5 77.0 reduce-scatter.27
  1017.0 137.8 reduce-scatter.23
  1158.0 22.0 reduce-scatter.31
  1182.6 120.0 reduce-scatter.33
  1306.2 69.5 reduce-scatter.29
  1379.2 94.8 reduce-scatter.25
where the time goes:
time: 1490 us; the launch traced here: 1480 us
  waiting for transfers between devices  1110 us (74%)
  matrix products  145 us (10%)
  local copies, waits for them, and re-layouts  85.5 us (6%)
  blocking collectives  68.7 us (5%)
  other arithmetic  46.1 us (3%)
  between operations  15.6 us (1%)
    reduce_scatter x1, waiting for transfers between devices, body(): lax.psum_scatter(grad_keys_all.astype(jnp.bfloat16), 'blk', scatter_dimen...  172 us
    unnamed x16, waiting for transfers between devices  122 us
    reduce_scatter x1, waiting for transfers between devices, body(): lax.psum_scatter(qkv_term.astype(jnp.bfloat16), 'sp', scatter_dimension=0...  115 us
    all_gather x1, waiting for transfers between devices, body(): lax.all_gather(act_ffn, 'blk', axis=0, tiled=True)  102 us
    reduce_scatter x1, waiting for transfers between devices, body(): lax.psum_scatter(qkv_part.astype(jnp.bfloat16), 'blk', scatter_dimension=...  96.6 us
    reduce_scatter x1, waiting for transfers between devices, body(): lax.psum_scatter(jnp.dot(part, w_down, preferred_element_type=jnp.float32...  94.1 us
    reduce_scatter x1, waiting for transfers between devices, body(): lax.psum_scatter(jnp.einsum('tkf,fkd->td', part, w_in, preferred_element_...  94.1 us
    all_gather x1, waiting for transfers between devices, body(): grad_piece = lax.all_gather(grad_ffn, 'blk', axis=0, tiled=True)  78.7 us
  transfers between devices with their start and end apart: 15, of which 14 were waited for; matrix products, arithmetic and copies ran while one was open for 8% of the time, Pallas kernels for 0%

commit v1 on v0

--- a/solution.py
+++ b/solution.py
@@ -161,8 +161,11 @@
     grad_out = cotangent.astype(jnp.float32)
     grad_ffn_f, gain_grad3 = norm_back(grad_out, normed_ffn, inverse_ffn, gains[3])
     grad_ffn = grad_ffn_f.astype(jnp.bfloat16)
-    act_piece = lax.all_gather(act_ffn, "blk", axis=0, tiled=True)
-    grad_piece = lax.all_gather(grad_ffn, "blk", axis=0, tiled=True)
+    act_piece, grad_piece = jnp.split(
+        lax.all_gather(jnp.concatenate([act_ffn, grad_ffn], axis=1), "blk", axis=0, tiled=True),
+        [act_ffn.shape[1]],
+        axis=1,
+    )
     gate_up = jnp.einsum("td,fkd->tkf", act_piece, w_in, preferred_element_type=jnp.float32)
     hidden = (gelu_value(gate_up[:, 0]) * gate_up[:, 1]).astype(jnp.bfloat16)
     grad_hidden = contract_last(grad_piece, w_down)

time: 1490 us -> 1570 us (1.054)
  waiting for transfers between devices: 1110 us -> 1170 us
  matrix products: 145 us -> 164 us
    all_gather x1, waiting for transfers between devices: 78.7 us -> 137 us  [body(): lax.all_gather(jnp.concatenate([act_ffn, grad_ffn], axis=1), 'blk', axis=...]
    dot_general x0 -> x1, matrix products: none -> 18.8 us  [body(): jnp.einsum('td,fkd->tkf', act_piece, w_in, preferred_element_type=jnp.flo...]
    unnamed x63 -> x67, local copies, waits for them, and re-layouts: 51.7 us -> 47.6 us
where the time goes in v1:
time: 1570 us; the launch traced here: 1550 us
  waiting for transfers between devices  1170 us (75%)
  matrix products  164 us (10%)
  local copies, waits for them, and re-layouts  79.2 us (5%)
  blocking collectives  68.5 us (4%)
  other arithmetic  45.2 us (3%)
    reduce_scatter x1, waiting for transfers between devices, body(): lax.psum_scatter(grad_keys_all.astype(jnp.bfloat16), 'blk', scatter_dimen...  171 us
    all_gather x1, waiting for transfers between devices, body(): lax.all_gather(jnp.concatenate([act_ffn, grad_ffn], axis=1), 'blk', axis=...  137 us
    unnamed x16, waiting for transfers between devices  123 us
    reduce_scatter x1, waiting for transfers between devices, body(): lax.psum_scatter(qkv_term.astype(jnp.bfloat16), 'sp', scatter_dimension=0...  116 us
    all_gather x1, waiting for transfers between devices, body(): lax.all_gather(act_ffn, 'blk', axis=0, tiled=True)  102 us
    reduce_scatter x1, waiting for transfers between devices, body(): lax.psum_scatter(qkv_part.astype(jnp.bfloat16), 'blk', scatter_dimension=...  96.6 us
    reduce_scatter x1, waiting for transfers between devices, body(): lax.psum_scatter(jnp.dot(part, w_down, preferred_element_type=jnp.float32...  94.1 us
    reduce_scatter x1, waiting for transfers between devices, body(): lax.psum_scatter(jnp.einsum('tkf,fkd->td', part, w_in, preferred_element_...  94 us
  transfers between devices with their start and end apart: 15, of which 14 were waited for; matrix products, arithmetic and copies ran while one was open for 8% of the time, Pallas kernels for 0%

profile of v1, /device:TPU:0, one launch (start us, length us, event | category | flops | bytes accessed | tf_op | source)
XLA Modules:
  0.0 1554.2 jit_solution(6311787223560806530)
XLA Ops:
  9.5 12.8 convolution_convert_fusion.5
  23.5 18.5 %all_to_all.57 = bf16[128,4,4,256]{3,2,0,1:T(4,128)(2,1)S(1)} all-to-all(bf16[128,4,4,256]{3,2,0,1:T(4,128)(2,1)S(1)} %copy.95), channel_id=1, replica_groups=mesh['blk'=8,'sp'=4] {'sp'}, dimensions={1} | all-to-all | bytes 2097152 | tf_op jit(solution)/shard_map/all_to_all | solution.py:65
  43.9 48.7 %all-gather.13.cloned.1.call-done = bf16[4096,1,1,256]{3,0,2,1:T(8,128)(2,1)} async-done(((bf16[512,1,1,256]{3,0,2,1:T(8,128)(2,1)}), bf16[4096,1,1,256]{3,0,2,1:T(8,128)(2,1)}) %all-gather.13.cloned.1.call-update) | async-done | bytes 2097168 | tf_op jit(solution)/shard_map/all_gather | solution.py:127
  96.5 46.4 %all-gather.11.cloned.1.call-done = bf16[4096,1,1,256]{3,0,2,1:T(8,128)(2,1)} async-done(((bf16[512,1,1,256]{3,0,2,1:T(8,128)(2,1)}), bf16[4096,1,1,256]{3,0,2,1:T(8,128)(2,1)}) %all-gather.11.cloned.1.call-update) | async-done | bytes 2097168 | tf_op jit(solution)/shard_map/all_gather | solution.py:126
  143.1 13.9 while.28
  159.4 11.3 all_to_all.58
  178.2 102.1 %all-gather.7.cloned.1.call-done = bf16[1024,2304]{1,0:T(8,128)(2,1)} async-done(((bf16[128,2304]{1,0:T(8,128)(2,1)}), bf16[1024,2304]{1,0:T(8,128)(2,1)}) %all-gather.7.cloned.1.call-update) | async-done | bytes 4718608 | tf_op jit(solution)/shard_map/all_gather | solution.py:146
  280.3 16.6 %fusion.53 = f32[1024,2,1152]{2,0,1:T(8,128)S(1)} fusion(bf16[1152,3,2304]{2,0,1:T(8,128)(2,1)} %param.18, bf16[1024,2304]{1,0:T(8,128)(2,1)} %all-gather.7.cloned.1.call-done), kind=kOutput, calls=%fused_computation.75 | convolution fusion | flops 10871635968 | bytes 24772608 | tf_op jit(solution)/shard_map/td,fkd->tkf/dot_general | solution.py:144
  296.9 11.3 convolution_convert_fusion.4
  308.2 94.1 %reduce-scatter.16.cloned.1.call-done = bf16[128,2304]{1,0:T(8,128)(2,1)} async-done(((bf16[1024,2304]{1,0:T(8,128)(2,1)}), bf16[128,2304]{1,0:T(8,128)(2,1)}) %reduce-scatter.16.cloned.1.call-update) | async-done | bytes 589840 | tf_op jit(solution)/shard_map/reduce_scatter | solution.py:153
  408.3 136.6 %all-gather.9.cloned.1.call-done = bf16[1024,4608]{1,0:T(8,128)(2,1)} async-done(((bf16[128,4608]{1,0:T(8,128)(2,1)}), bf16[1024,4608]{1,0:T(8,128)(2,1)}) %all-gather.9.cloned.1.call-update) | async-done | bytes 9437200 | tf_op jit(solution)/shard_map/all_gather | solution.py:165
  544.9 18.8 %fusion.56 = f32[1024,2,1152]{2,0,1:T(8,128)} fusion(bf16[1152,3,2304]{2,0,1:T(8,128)(2,1)} %param.18, bf16[1024,4608]{1,0:T(8,128)(2,1)} %all-gather.9.cloned.1.call-done), kind=kOutput, calls=%fused_computation.76 | convolution fusion | flops 10871635968 | bytes 24772608 | tf_op jit(solution)/shard_map/td,fkd->tkf/dot_general | solution.py:169
  563.7 13.6 fusion.88
  578.8 15.6 %bitcast_convert_fusion = bf16[1024,2304]{1,0:T(8,128)(2,1)} fusion(bf16[1152,3,2304]{2,0,1:T(8,128)(2,1)} %param.18, bf16[1024,1,1152]{2,0,1:T(8,128)(2,1)} %get-tuple-element.544, bf16[1024,1,1152]{2,0,1:T(8,128)(2,1)S(1)} %get-tuple-element.543), kind=kOutput, calls=%fused_computation.65 | convolution fusion | flops 10876354560 | bytes 20054016 | tf_op jit(solution)/shard_map/tkf,fkd->td/dot_general | solution.py:180
  594.4 94.0 %reduce-scatter.18.cloned.1.call-done = bf16[128,2304]{1,0:T(8,128)(2,1)} async-done(((bf16[1024,2304]{1,0:T(8,128)(2,1)}), bf16[128,2304]{1,0:T(8,128)(2,1)}) %reduce-scatter.18.cloned.1.call-update) | async-done | bytes 589840 | tf_op jit(solution)/shard_map/reduce_scatter | solution.py:179
  705.8 8.6 all-to-all-done.2
  722.4 26.5 %while.29 = (s32[]{:T(128)}, f32[512,1,2,256]{0,3,2,1:T(8,128)S(1)}, f32[4096,1,256]{2,0,1:T(8,128)}, f32[4096,1,256]{2,0,1:T(8,128)}, s32[8]{0:T(128)S(1)}, /*i...) while((s32[]{:T(128)}, ...), condition=%wide.region_18.19_spmd.clone, body=%wide.region_15.18_spmd.clone.sunk | while | flops 1350304768 | bytes 27805592 | solution.py:98
  723.6 16.7 %conditional.7 = ((f32[512,1,2,256]{0,3,2,1:T(8,128)S(1)}, f32[4096,1,256]{2,0,1:T(8,128)}, f32[4096,1,256]{2,0,1:T(8,128)})) conditional(s32[]{:T(128)} %convert_element_type.314, (f32[512,1,2,256]{0,3,2,1:T(8,128)S(1)}, f32[4096,1,256]{2,0,1:T(8,128)}, f32[4096,1,256]{2,0,1:T(8,128)}) %tuple.108, (bf16[8,512,1,256]{3,1,2,0:T(8,128)(2,1)}, ...), branch_computations={%region_16.16_spmd, %region_17.17_spmd} | conditional | flops 1350304768 | bytes 27803254 | solution.py:241
  763.5 171.0 %reduce-scatter.20.cloned.1.call-done = bf16[512,1,256]{2,0,1:T(8,128)(2,1)} async-done(((bf16[4096,1,256]{2,0,1:T(8,128)(2,1)}), bf16[512,1,256]{2,0,1:T(8,128)(2,1)}) %reduce-scatter.20.cloned.1.call-update) | async-done | bytes 262160 | tf_op jit(solution)/shard_map/reduce_scatter | solution.py:259
  935.8 70.2 %reduce-scatter.22.cloned.1.call-done = bf16[512,1,256]{2,0,1:T(8,128)(2,1)} async-done(((bf16[4096,1,256]{2,0,1:T(8,128)(2,1)}), bf16[512,1,256]{2,0,1:T(8,128)(2,1)}) %reduce-scatter.22.cloned.1.call-update) | async-done | bytes 262160 | tf_op jit(solution)/shard_map/reduce_scatter | solution.py:262
  1009.1 17.0 %all_to_all.59 = bf16[512,1,4,256]{3,2,1,0:T(4,128)(2,1)S(1)} all-to-all(bf16[512,1,4,256]{3,2,1,0:T(4,128)(2,1)S(1)} %pad_maximum_fusion.5), channel_id=1, replica_groups=mesh['blk'=8,'sp'=4] {'sp'}, dimensions={0} | all-to-all | bytes 2097152 | tf_op jit(solution)/shard_map/all_to_all | solution.py:269
  1027.2 9.4 convolution_convert_fusion
  1036.7 13.2 fusion.46
  1049.9 17.4 %fusion.45 = bf16[1152,2,2304]{0,2,1:T(8,128)(2,1)} fusion(bf16[1024,4608]{1,0:T(8,128)(2,1)} %all-gather.9.cloned.1.call-done, bf16[1024,1,1152]{2,0,1:T(8,128)(2,1)} %get-tuple-element.544, bf16[1024,1,1152]{2,0,1:T(8,128)(2,1)} %copy-done.24), kind=kOutput, calls=%fused_computation.61 | convolution fusion | flops 10886381568 | bytes 20054016 | tf_op jit(solution)/shard_map/tkf,td->fkd/dot_general | solution.py:175
  1073.9 13.4 pad_maximum_fusion
  1087.3 21.6 %copy.131 = bf16[1152,6912]{1,0:T(8,128)(2,1)} copy(bf16[1152,6912]{0,1:T(8,128)(2,1)} %bitcast.248) | data formatting | bytes 31850496
  1109.8 116.0 %reduce-scatter.24.cloned.1.call-done = bf16[1024,2304]{1,0:T(8,128)(2,1)} async-done(((bf16[4096,2304]{1,0:T(8,128)(2,1)}), bf16[1024,2304]{1,0:T(8,128)(2,1)}) %reduce-scatter.24.cloned.1.call-update) | async-done | bytes 4718608 | tf_op jit(solution)/shard_map/reduce_scatter | solution.py:282
  1228.9 22.0 %reduce-scatter.32.cloned.1.call-done = bf16[576,4]{1,0:T(8,128)(2,1)} async-done(((bf16[2304,4]{1,0:T(8,128)(2,1)}), bf16[576,4]{1,0:T(8,128)(2,1)}) %reduce-scatter.32.cloned.1.call-update) | async-done | bytes 4624
  1251.9 21.7 %all-reduce = bf16[4,576]{1,0:T(4,128)(2,1)S(1)} all-reduce(bf16[4,576]{1,0:T(4,128)(2,1)S(1)} %copy.126), channel_id=13, replica_groups=mesh['blk'=8,'sp'=4] {'blk'}, use_global_device_ids=true, to_apply=%region_31.32.clone | all-reduce | flops 2304 | bytes 9216
  1274.3 99.2 %reduce-scatter.34.cloned.1.call-done = bf16[288,6912]{1,0:T(8,128)(2,1)} async-done(((bf16[1152,6912]{1,0:T(8,128)(2,1)}), bf16[288,6912]{1,0:T(8,128)(2,1)}) %reduce-scatter.34.cloned.1.call-update) | async-done | bytes 3981328
  1387.4 59.3 %reduce-scatter.30.cloned.1.call-done = bf16[64,2304]{1,0:T(8,128)(2,1)} async-done(((bf16[512,2304]{1,0:T(8,128)(2,1)}), bf16[64,2304]{1,0:T(8,128)(2,1)}) %reduce-scatter.30.cloned.1.call-update) | async-done | bytes 294928 | tf_op jit(solution)/shard_map/reduce_scatter | solution.py:296
  1448.5 96.6 %reduce-scatter.26.cloned.1.call-done = bf16[128,2304]{1,0:T(8,128)(2,1)} async-done(((bf16[1024,2304]{1,0:T(8,128)(2,1)}), bf16[128,2304]{1,0:T(8,128)(2,1)}) %reduce-scatter.26.cloned.1.call-update) | async-done | bytes 589840 | tf_op jit(solution)/shard_map/reduce_scatter | solution.py:293
  (222 shorter events, 134.7 us)
Async XLA Ops:
  7.2 85.4 %all-gather.13.cloned.1.call-start = ((), (), s32[]{:S(2)}) async-start(), calls=%async_computation.25 | async-start | bytes 2359296 | tf_op jit(solution)/shard_map/all_gather | solution.py:127
  8.2 14.1 copy-start.18
  9.5 12.8 copy-start.20
  43.0 99.9 %all-gather.11.cloned.1.call-start = ((), (), s32[]{:S(2)}) async-start(), calls=%async_computation.24 | async-start | bytes 2359296 | tf_op jit(solution)/shard_map/all_gather | solution.py:126
  43.8 236.5 %all-gather.7.cloned.1.call-start = ((), (), s32[]{:S(2)}) async-start(), calls=%async_computation.14 | async-start | bytes 5308416 | tf_op jit(solution)/shard_map/all_gather | solution.py:146
  171.1 5.4 copy-start.8
  171.1 5.4 copy-start.1
  177.9 224.4 %reduce-scatter.16.cloned.1.call-start = ((), (), s32[]{:S(2)}) async-start(), calls=%async_computation.15 | async-start | bytes 5308416 | tf_op jit(solution)/shard_map/reduce_scatter | solution.py:153
  308.2 95.5 %copy-start.12 = (bf16[128,2304]{1,0:T(8,128)(2,1)S(1)}, bf16[128,2304]{1,0:T(8,128)(2,1)}, u32[]{:S(2)}) copy-start(bf16[128,2304]{1,0:T(8,128)(2,1)} %param.19) | copy-start | bytes 1769476
  308.2 236.7 %all-gather.9.cloned.1.call-start = ((), (), s32[]{:S(2)}) async-start(), calls=%async_computation.16 | async-start | bytes 10616832 | tf_op jit(solution)/shard_map/all_gather | solution.py:165
  402.3 4.3 copy-start.13
  407.8 280.6 %reduce-scatter.18.cloned.1.call-start = ((), (), s32[]{:S(2)}) async-start(), calls=%async_computation.17 | async-start | bytes 5308416 | tf_op jit(solution)/shard_map/reduce_scatter | solution.py:179
  544.9 18.8 %copy-start.22 = (bf16[1024,4608]{1,0:T(8,128)(2,1)S(1)}, bf16[1024,4608]{1,0:T(8,128)(2,1)}, u32[]{:S(2)}) copy-start(bf16[1024,4608]{1,0:T(8,128)(2,1)} %all-gather.9.cloned.1.call-done) | copy-start | bytes 28311556
  594.4 95.5 %copy-start.7 = (bf16[128,2304]{1,0:T(8,128)(2,1)S(1)}, bf16[128,2304]{1,0:T(8,128)(2,1)}, u32[]{:S(2)}) copy-start(bf16[128,2304]{1,0:T(8,128)(2,1)} %reduce-scatter.16.cloned.1.call-done) | copy-start | bytes 1769476
  694.2 7.0 copy-start.10
  701.2 13.7 copy-start.15
  701.3 13.7 copy-start.17
  702.1 12.3 all-to-all-start.2
  705.6 228.9 %reduce-scatter.20.cloned.1.call-start = ((), (), s32[]{:S(2)}) async-start(), calls=%async_computation.18 | async-start | bytes 2359296 | tf_op jit(solution)/shard_map/reduce_scatter | solution.py:259
  752.6 253.4 %reduce-scatter.22.cloned.1.call-start = ((), (), s32[]{:S(2)}) async-start(), calls=%async_computation.19 | async-start | bytes 2359296 | tf_op jit(solution)/shard_map/reduce_scatter | solution.py:262
  756.4 352.7 %reduce-scatter.28.cloned.1.call-start = ((), (), s32[]{:S(2)}) async-start(), calls=%async_computation.22 | async-start | bytes 11796480 | tf_op jit(solution)/shard_map/reduce_scatter | solution.py:285
  762.6 463.2 %reduce-scatter.24.cloned.1.call-start = ((), (), s32[]{:S(2)}) async-start(), calls=%async_computation.20 | async-start | bytes 23592960 | tf_op jit(solution)/shard_map/reduce_scatter | solution.py:282
  1026.9 9.7 copy-start.4
  1036.6 214.3 %reduce-scatter.32.cloned.1.call-start = ((), (), s32[]{:S(2)}) async-start(), calls=%async_computation.26 | async-start | bytes 737280
  1036.7 30.6 %slice-start = ((s8[18874368]{0:T(1024)(128)(4,1)}), s8[4194304]{0:T(1024)(128)(4,1)S(1)}, s32[]{:S(2)}) async-start(s8[18874368]{0:T(1024)(128)(4,1)} %bitcast.246), calls=%async_computation.28 | async-start | bytes 8388608
  1036.7 30.6 %slice-start.1 = ((s8[18874368]{0:T(1024)(128)(4,1)}), s8[4194304]{0:T(1024)(128)(4,1)S(1)}, s32[]{:S(2)}) async-start(s8[18874368]{0:T(1024)(128)(4,1)} %bitcast.246), calls=%async_computation.29 | async-start | bytes 8388608
  1049.9 17.4 %slice-start.2 = ((s8[18874368]{0:T(1024)(128)(4,1)}), s8[4194304]{0:T(1024)(128)(4,1)S(1)}, s32[]{:S(2)}) async-start(s8[18874368]{0:T(1024)(128)(4,1)} %bitcast.246), calls=%async_computation.30 | async-start | bytes 8388608
  1049.9 17.4 %slice-start.3 = ((s8[18874368]{0:T(1024)(128)(4,1)}), s8[4194304]{0:T(1024)(128)(4,1)S(1)}, s32[]{:S(2)}) async-start(s8[18874368]{0:T(1024)(128)(4,1)} %bitcast.246), calls=%async_computation.31 | async-start | bytes 8388608
  1049.9 17.4 %slice-start.4 = ((s8[18874368]{0:T(1024)(128)(4,1)}), s8[2097152]{0:T(1024)(128)(4,1)S(1)}, s32[]{:S(2)}) async-start(s8[18874368]{0:T(1024)(128)(4,1)} %bitcast.246), calls=%async_computation.32 | async-start | bytes 4194304
  1073.8 299.6 %reduce-scatter.34.cloned.1.call-start = ((), (), s32[]{:S(2)}) async-start(), calls=%async_computation.27 | async-start | bytes 19906560
  1109.0 337.7 %reduce-scatter.30.cloned.1.call-start = ((), (), s32[]{:S(2)}) async-start(), calls=%async_computation.23 | async-start | bytes 2654208 | tf_op jit(solution)/shard_map/reduce_scatter | solution.py:296
  1109.7 435.4 %reduce-scatter.26.cloned.1.call-start = ((), (), s32[]{:S(2)}) async-start(), calls=%async_computation.21 | async-start | bytes 5308416 | tf_op jit(solution)/shard_map/reduce_scatter | solution.py:293
  (13 other events, 17.8 us)
Sparse Core Ops, SparseCore 0:
  43.2 49.3 all-gather.12
  95.3 47.6 all-gather.10
  178.1 102.1 all-gather.6
  308.3 93.9 reduce-scatter.15
  407.9 136.8 all-gather.8
  594.6 93.7 reduce-scatter.17
  752.7 181.6 reduce-scatter.19
  938.5 67.4 reduce-scatter.21
  1008.6 76.8 reduce-scatter.27
  1087.9 137.8 reduce-scatter.23
  1228.8 22.0 reduce-scatter.31
  1253.4 120.0 reduce-scatter.33
  1377.0 69.6 reduce-scatter.29
  1450.2 94.8 reduce-scatter.25
